TPU v7x, 32 devices: a 4x2x2 block of a 4x4x8 slice. The times are simulated.
32 devices in a mesh: seqs: 4 (over y, z), states: 8 (over x, core).
Axes of the slice: x: 4, y: 2, z: 2, core: 2. Of those that a mesh axis runs over, the one named last changes fastest.
The devices are a block of a 4x4x8 slice.
Arguments:
- trans_mat: bfloat16 [16384, 16384], P(None, 'states')
- emit_mat: bfloat16 [16384, 10000], P('states')
- init_prob: float32 [16384], P('states')
- tokens: int32 [512, 8], P('seqs'), parts along dimension 0
- lengths: int32 [512], P('seqs'), parts along dimension 0
Outputs:
- output 1: float32 [512], P('seqs'), parts along dimension 0
- output 2: float32 [512, 16384], P('seqs', 'states'), parts along dimension 0
- output 3: float32 [65536, 2048], P(('seqs', 'states')), parts along dimension 0
There are 4 independent parts. A program takes and returns all parts, laid end to end along the dimension named above; an argument that names none is the same for every part.
All inputs are finite; a program needn't handle non-finite values.
Results may differ from a plain program's by a relative error of at most 0.001.
Values are sent between devices in bfloat16 or wider.
A program may use at most 768 MiB of HBM per device.

v0:
```python
import functools
import math

import jax
import jax.numpy as jnp
from jax import lax
from jax.experimental import pallas as pl
from jax.experimental.pallas import tpu as pltpu
from jax.sharding import PartitionSpec as P

AXIS = "states"
LANES = 128
BOTH = (0, 1)
F32 = jnp.float32
BF16 = jnp.bfloat16


def _dot(a, b, over_a=1, over_b=0):
    dims = (((over_a,), (over_b,)), ((), ()))
    return lax.dot_general(a, b, dims, preferred_element_type=F32)


def _start(copies):
    for cp in copies:
        cp.start()


def _wait(copies):
    for cp in copies:
        cp.wait()


def _loop(n, body):
    def step(i, carry):
        body(i)
        return carry

    lax.fori_loop(0, n, step, 0)


def _recursion(caps, a_hbm, em_hbm, pi_ref, lcol_ref, lrow_ref, al_hbm, w_hbm, post_hbm, ll_ref, turned_hbm,
               bank, al, work, emv, rcs, sbuf, csend, cbuf, strips, ost, dbuf, trans, fin,
               bank_sem, em_sem, al_recv, own_send, part_send, on_send, c_send, c_recv, save_sem, post_sem,
               strip_sem, d_send, d_recv, s_send, t_recv, f_recv, t_free, f_free, d_free):
    nd = cbuf.shape[0]
    nx = nd // 2
    step_count, seqs, bs = em_hbm.shape
    hb = bs // 2
    firsts = [sum(caps[:t]) for t in range(step_count)]
    slab = min(512, hb)
    tiles = bs // LANES
    kept = max(caps[1:])
    sent = pl.ds(0, kept)
    final = step_count - 1
    g = lax.axis_index(AXIS)
    x, c = g // 2, g % 2

    def dev(dx, flip):
        return ((x + dx) % nx) * 2 + (c + flip) % 2

    partner, right, left = dev(0, 1), dev(1, 0), dev(nx - 1, 0)

    def remote(src, dst, send, recv, to):
        return pltpu.make_async_remote_copy(
            src_ref=src, dst_ref=dst, send_sem=send, recv_sem=recv,
            device_id={AXIS: to}, device_id_type=pl.DeviceIdType.MESH)

    def pick(t, fn, lo, hi):
        if hi - lo == 1:
            fn(lo)
        else:
            mid = (lo + hi) // 2
            lax.cond(t < mid, lambda: pick(t, fn, lo, mid), lambda: pick(t, fn, mid, hi))

    def for_each(t, fn):
        pick(t, lambda tt: fn(tt, caps[tt - 1]), 1, step_count)

    def for_caps(t, fn, first=1):
        if len(set(caps)) == 1:
            fn(caps[0])
        else:
            pick(t, lambda tt: fn(caps[tt - 1]), first, step_count)

    acc, cur = work.at[pl.ds(0, 2)], work.at[pl.ds(4, 2)]

    def tile_row(group, i):
        if group == 0:
            src, half = dev(0, i // 2), i % 2
        elif group == 1:
            src, half = dev(nx - 1, i % 2), i // 2
        elif group == 2:
            src, half = dev(1, i % 2), 1 - i // 2
        else:
            src, half = dev(2, i // 2), i % 2
        return src * bs + half * hb

    def load(slot, row, src):
        pltpu.make_async_copy(src.at[pl.ds(pl.multiple_of(row, hb), hb)], bank.at[slot], bank_sem.at[slot]).start()

    def load_tile(slot, group, i):
        load(slot, tile_row(group, i), a_hbm)

    def load_turned(slot, number):
        load(slot, number * hb, turned_hbm)

    def in_bank(slot):
        pltpu.make_async_copy(a_hbm.at[pl.ds(0, hb)], bank.at[slot], bank_sem.at[slot]).wait()

    depth = strips.shape[0]
    bunch = min(2, depth)

    def strip_copy(number, unit, k):
        rows = pl.ds(pl.multiple_of(number * hb + (unit % (tiles // 2)) * LANES, LANES), LANES)
        cols = pl.ds(pl.multiple_of((unit // (tiles // 2)) * hb, hb), hb)
        return pltpu.make_async_copy(strips.at[k], turned_hbm.at[rows, cols], strip_sem.at[k])

    def turn(slot, number, first):
        def body(i):
            units = [bunch * i + e for e in range(bunch)]

            @pl.when(jnp.logical_not(first) | (bunch * i >= depth))
            def _():
                for u in units:
                    strip_copy(0, 0, u % depth).wait()

            for u in units:
                strips[u % depth] = jnp.transpose(bank[slot, :, pl.ds(pl.multiple_of(u * LANES, LANES), LANES)])
            for u in units:
                strip_copy(number, u, u % depth).start()

        _loop(tiles // bunch, body)

    own_each, other_each = -(-7 // final), -(-5 // (final - 1))

    def turn_own(t):
        each = own_each

        def body(e):
            n = t * each + e
            far = n // 4
            pl.when(far == 0)(lambda: in_bank(8 + n))
            pl.when(n < 7)(lambda: turn(8 + n - far * 7, n + far * 9, n == 0))

        _loop(each, body)
        _loop(4, lambda i: pl.when((t > 0) & ((i < t * each) | (i >= t * each + each)))(lambda: in_bank(8 + i)))

    def turn_others(t):
        each = other_each

        def body(e):
            n = (t - 1) * each + e
            right = (e + LANES - each) // LANES
            slot = (1 - right) * n + right * (8 + e - each)
            number = (1 - right) * (4 + n + 4 * (n // 4)) + right * slot
            pl.when((right == 1) & (t == 1))(lambda: in_bank(slot))
            pl.when(((right == 1) & (t == 1)) | ((right == 0) & (n < 5)))(lambda: turn(slot, number, False))

        pl.when(t < final)(lambda: _loop(each + 2, body))

    def em_copy(t):
        return pltpu.make_async_copy(em_hbm.at[t], emv.at[t % 2], em_sem.at[t % 2])

    _loop(2, lambda t: em_copy(t).start())
    _loop(4, lambda i: load_tile(8 + i, 0, i))
    _loop(4, lambda i: load_tile(i, 1, i))

    barrier = pltpu.get_barrier_semaphore()
    for k in range(1, nd):
        pl.semaphore_signal(barrier, inc=1, device_id={AXIS: (g + k) % nd}, device_id_type=pl.DeviceIdType.MESH)
    pl.semaphore_wait(barrier, nd - 1)

    tall = 16

    def rows_of(i):
        return pl.ds(pl.multiple_of(i * tall, tall), tall)

    def eight(i):
        return pl.ds(pl.multiple_of(i * 8, 8), 8)

    def lane(k):
        return pl.ds(k * LANES, LANES)

    def inner(k):
        return (k * LANES) // hb, pl.ds((k * LANES) % hb, LANES)

    def weigh(t):
        def body(i):
            r = rows_of(i)
            total = jnp.zeros((tall, LANES), F32)
            for k in range(tiles):
                e = emv[t % 2, r, lane(k)].astype(F32)
                h, col = inner(k)
                mass = acc[h, r, col] * e
                acc[h, r, col] = mass
                total = total + mass
            sbuf[r, :] = total

        _loop(seqs // tall, body)

    def normalise(t):
        row = jnp.sum(jnp.transpose(sbuf[...]), axis=0, keepdims=True)
        wide = jnp.broadcast_to(row, csend.shape)
        csend[...] = wide
        cbuf[g] = wide
        peers = [dev(dx, flip) for dx in (2, 1, nx - 1, 0) for flip in BOTH][: nd - 2] + [partner]
        copies = [remote(csend, cbuf.at[g], c_send.at[k], c_recv.at[g], to) for k, to in enumerate(peers)]
        _start(copies)

        with jax.named_scope("ft"):
            @pl.when(t < final)
            def _():
                turn_own(t)

        with jax.named_scope("fx"):
            for k, frm in enumerate(peers):
                remote(csend, cbuf.at[frm], c_send.at[k], c_recv.at[frm], frm).wait_recv()
        norm = cbuf[0, 0:1, :]
        for d in range(1, nd):
            norm = norm + cbuf[d, 0:1, :]
        rcs[t] = 1.0 / jnp.transpose(jnp.broadcast_to(norm, (LANES, LANES)))
        ll_ref[...] = ll_ref[...] + jnp.where(t < lrow_ref[...], jnp.log(jnp.broadcast_to(norm, ll_ref.shape)), 0.0)

        def body(i):
            r = rows_of(i)
            rc = rcs[t, r, :]
            live = t < lcol_ref[r, :]
            for k in range(tiles):
                h, col = inner(k)
                val = jnp.where(live, acc[h, r, col] * rc, cur[h, r, col])
                cur[h, r, col] = val
                al[0, h, r, col] = val.astype(BF16)

        _loop(seqs // tall, body)
        for cp in copies:
            cp.wait_send()

    ll_ref[...] = jnp.zeros_like(ll_ref)
    for h in BOTH:
        acc[h] = jnp.broadcast_to(pi_ref[:, h * hb : (h + 1) * hb], (seqs, hb))

    def own_copies(rows):
        m = pl.ds(0, rows)
        out = [remote(al.at[0, h, m], al.at[1, h, m], own_send.at[0, h], al_recv.at[1, h], partner) for h in BOTH]
        for h in BOTH:
            out.append(remote(al.at[0, h, m], al.at[2, h, m], own_send.at[1, h], al_recv.at[2, h], right))
            out.append(remote(al.at[0, 1 - h, m], al.at[3, 1 - h, m], own_send.at[2, 1 - h], al_recv.at[3, 1 - h], left))
        return out

    def to_partner(slot, to_slot, half, rows):
        m = pl.ds(0, rows)
        return remote(al.at[slot, half, m], al.at[to_slot, half, m], part_send.at[slot, half], al_recv.at[to_slot, half], partner)

    def onward(s, rows):
        m = pl.ds(0, rows)
        return remote(al.at[2 + s, s, m], al.at[6, s, m], on_send.at[s], al_recv.at[6, s], dev(1 + (nx - 2) * s, 0))

    def arrived(slot, half, rows):
        m = pl.ds(0, rows)
        remote(al.at[slot, half, m], al.at[slot, half, m], part_send.at[slot, half], al_recv.at[slot, half], partner).wait_recv()

    def save_copies(t, rows):
        to = pl.ds(firsts[t - 1], rows)
        return [pltpu.make_async_copy(al.at[0, h, pl.ds(0, rows)], al_hbm.at[to, pl.ds(h * hb, hb)], save_sem.at[h])
                for h in BOTH]

    def multiply(one, two):
        (slot1, half1, tile1), (slot2, half2, tile2) = one, two
        lhs1, lhs2 = al[slot1, half1], al[slot2, half2]
        for h in BOTH:
            for n in range(hb // slab):
                cols, at = pl.ds(h * hb + n * slab, slab), pl.ds(n * slab, slab)
                acc[h, :, at] = acc[h, :, at] + (
                    _dot(lhs1, tile1[:, cols]) + _dot(lhs2, tile2[:, cols]))

    def forward(t):
        pl.when(t > 0)(lambda: predict(t))
        em_copy(t).wait()
        with jax.named_scope("fw"):
            weigh(t)
        normalise(t)

    def predict(t):
        for_caps(t, lambda rows: _start(own_copies(rows)))
        for_each(t, lambda tt, rows: _start(save_copies(tt, rows)))

        @pl.when(t + 1 < step_count)
        def _():
            em_copy(t + 1).start()

        acc[...] = jnp.zeros(acc.shape, F32)

        def group0(j):
            def ready(rows):
                for half in BOTH:
                    arrived(1, half, rows)

            pl.when(j > 0)(lambda: for_caps(t, ready))
            _loop(2, lambda e: pl.when((t == 1) & (2 * j + e >= own_each))(lambda: in_bank(8 + 2 * j + e)))
            multiply(*((j, e, bank.at[8 + 2 * j + e]) for e in BOTH))
            for e in BOTH:
                load_tile(8 + 2 * j + e, 2, 2 * j + e)

        def group12(k, j):
            def ready(rows):
                arrived(2 + 2 * j, k, rows)
                arrived(3 + 2 * j, 1 - k, rows)

                @pl.when(j == 0)
                def _():
                    to_partner(2, 4, k, rows).start()
                    to_partner(3, 5, 1 - k, rows).start()

                pl.when(k + j == 0)(lambda: _start([onward(0, rows), onward(1, rows)]))

            for_caps(t, ready)
            at = 2 * k + j
            pl.when((t > 1) | (at > 1))(lambda: in_bank(8 + at))
            pl.when((t == 1) & (at >= other_each))(lambda: in_bank(at))
            multiply((2 + 2 * j, k, bank.at[at]), (3 + 2 * j, 1 - k, bank.at[8 + at]))

        def next_tiles(k):
            def body(e):
                i = 2 * k + e
                pl.when(t < final)(lambda: load_tile(8 + i, 0, i))

                @pl.when(t == final)
                def _():
                    load_turned(8 + i, 12 + i)
                    load_turned(i, 4 + i)

            _loop(2, body)

        def group3(j):
            def ready(rows):
                for half in BOTH:
                    arrived(6 + j, half, rows)

                @pl.when(j == 0)
                def _():
                    for half in BOTH:
                        to_partner(6, 7, half, rows).start()

            for_caps(t, ready)
            multiply(*((6 + j, e, bank.at[4 + 2 * j + e]) for e in BOTH))

        with jax.named_scope("f0"):
            _loop(2, group0)

        @pl.when(t == 1)
        def _():
            _loop(4, lambda i: load_tile(4 + i, 3, i))
            _loop(other_each, in_bank)

        with jax.named_scope("ft"):
            turn_others(t)
        pl.when(t == final)(lambda: _loop(depth, lambda k: strip_copy(0, 0, k).wait()))

        def groups12(k):
            with jax.named_scope("f1"):
                _loop(2, functools.partial(group12, k))
            pl.when((k == 1) & (t > 1) & (t < 4))(lambda: turn(8 + t, 8 + t, False))
            next_tiles(k)

        _loop(2, groups12)
        pl.when(t == 1)(lambda: _loop(4, lambda i: in_bank(4 + i)))
        with jax.named_scope("f3"):
            _loop(2, group3)
        pl.when(t == final)(lambda: _loop(4, lambda i: load_turned(4 + i, 8 + i)))

        def drained(rows):
            for cp in own_copies(rows):
                cp.wait_send()
            for half in BOTH:
                to_partner(2, 4, half, rows).wait_send()
                to_partner(3, 5, half, rows).wait_send()
                to_partner(6, 7, half, rows).wait_send()
                onward(half, rows).wait_send()

        for_caps(t, drained)
        for_each(t, lambda tt, rows: _wait(save_copies(tt, rows)))

    _loop(step_count, forward)

    def post_copy(h):
        return pltpu.make_async_copy(cur.at[h], post_hbm.at[:, pl.ds(pl.multiple_of(h * hb, hb), hb)], post_sem.at[h])

    _loop(2, lambda h: post_copy(h).start())

    back_caps = functools.partial(for_caps, first=2)

    def weights(t):
        def body(i):
            r = eight(i)
            rc = rcs[t, r, :]
            live, later = t < lcol_ref[r, :], t + 1 < lcol_ref[r, :]
            for k in range(tiles):
                h, col = inner(k)
                beta = jnp.where(later, acc[h, r, col] + fin[0, h, r, col] + fin[1, h, r, col], 1.0)
                val = emv[t % 2, r, lane(k)].astype(F32) * beta * rc
                strips[h, r, col] = jnp.where(live, val, 0.0).astype(BF16)

        _loop(kept // 8, body)

    def w_copies(t, rows):
        to = pl.ds(firsts[t - 1], rows)
        return [pltpu.make_async_copy(strips.at[h, pl.ds(0, rows)], w_hbm.at[to, pl.ds(h * hb, hb)], save_sem.at[h])
                for h in BOTH]

    def partial_sums(out, tile):
        for n in range(hb // slab):
            cols = pl.ds(n * slab, slab)
            more = pl.ds(hb + n * slab, slab)
            out[sent, cols] = _dot(strips[0, sent, :], tile[:, cols]) + _dot(strips[1, sent, :], tile[:, more])

    def add_into(out, *terms):
        def body(i):
            r = eight(i)
            val = out[r, :]
            for term in terms:
                val = val + term[r, :]
            out[r, :] = val

        _loop(kept // 8, body)

    def to_core(q, rows):
        m = pl.ds(0, rows)
        return remote(ost.at[q, m], dbuf.at[q, m], d_send.at[q], d_recv.at[q], partner)

    def staged(p):
        n, q = p // 2, p % 2
        return (1 - n % 2) * (2 + n) + q

    def ring_copy(far, p, rows):
        m, q = pl.ds(0, rows), p % 2
        to = dev(1 + (nx - 2) * q, 0)
        src, send = work.at[staged(p), m], s_send.at[p]
        if far:
            return remote(src, trans.at[q, m], send, t_recv.at[q], to)
        half = (p // 2 + q) % 2
        return remote(src, fin.at[q, half, m], send, f_recv.at[q, half], to)

    def freed(sem, q):
        pl.semaphore_signal(sem.at[q], inc=1, device_id={AXIS: dev(nx - 1 - (nx - 2) * q, 0)},
                            device_id_type=pl.DeviceIdType.MESH)

    def backward(idx):
        t = step_count - 1 - idx
        with jax.named_scope("bw"):
            weights(t)
        _loop(2, functools.partial(freed, f_free))
        for_each(t, lambda tt, rows: _start(w_copies(tt, rows)))

        @pl.when(t > 2)
        def _():
            em_copy(t - 2).start()

        def slot_of(p, flip):
            n, q = p // 2, p % 2
            inner = ((n + 1) % 4) // 2
            return inner == 0, (1 - inner) * (8 + 2 * flip + q) + inner * (4 * (1 - q) + 2 * (n - 1) + flip)

        def products(n, flip, outs):
            outer, _ = slot_of(2 * n, flip)
            slots = [slot_of(2 * n + q, flip)[1] for q in BOTH]

            @pl.when(outer | (idx == 0))
            def _():
                for slot in slots:
                    in_bank(slot)

            for slot, out in zip(slots, outs):
                partial_sums(out, bank.at[slot])

            @pl.when(n == 0)
            def _():
                for slot in slots:
                    load_turned(slot, slot - 8)

            @pl.when((n == 3) & (t > 2))
            def _():
                for slot in slots:
                    load_turned(slot, slot + 4)

        def for_other(n):
            def drain(rows):
                for q in BOTH:
                    to_core(q, rows).wait_send()

            pl.when(n > 0)(lambda: back_caps(t, drain))
            products(n, 1, [ost.at[q] for q in BOTH])

            @pl.when((n > 0) | (idx > 0))
            def _():
                for q in BOTH:
                    pl.semaphore_wait(d_free.at[q], 1)

            back_caps(t, lambda rows: _start([to_core(q, rows) for q in BOTH]))

        def for_this(n):
            outs = [work.at[staged(2 * n + q)] for q in BOTH]
            pl.when((n == 2) & (idx == 0))(lambda: _wait([post_copy(q) for q in BOTH]))

            def drain(rows):
                for q in BOTH:
                    ring_copy(False, 2 + q, rows).wait_send()

            pl.when(n == 3)(lambda: back_caps(t, drain))
            products(n, 0, outs)
            for q, out in enumerate(outs):
                p = 2 * n + q
                back_caps(t, lambda rows: to_core(q, rows).wait_recv())

                @pl.when(n == 2)
                def _():
                    back_caps(t, lambda rows: ring_copy(True, q, rows).wait_recv())
                    add_into(out, dbuf.at[q], trans.at[q])
                    pl.when(t > 2)(lambda: freed(t_free, q))

                pl.when(n != 2)(lambda: add_into(out, dbuf.at[q]))

                @pl.when((n < 3) | (t > 2))
                def _():
                    pl.semaphore_signal(d_free.at[q], inc=1, device_id={AXIS: partner}, device_id_type=pl.DeviceIdType.MESH)

                @pl.when(n == 0)
                def _():
                    pl.when(idx > 0)(lambda: pl.semaphore_wait(t_free.at[q], 1))
                    back_caps(t, lambda rows: ring_copy(True, q, rows).start())

                @pl.when((n == 1) | (n == 2))
                def _():
                    pl.when(n == 1)(lambda: pl.semaphore_wait(f_free.at[q], 1))
                    back_caps(t, lambda rows: ring_copy(False, p, rows).start())

        def stage(n):
            with jax.named_scope("bo"):
                for_other(n)
            with jax.named_scope("bt"):
                for_this(n)

        _loop(4, stage)

        def landed(rows):
            for p in range(2, 6):
                ring_copy(False, p, rows).wait_recv()

        with jax.named_scope("bl"):
            back_caps(t, landed)

        def drained(rows):
            for q in BOTH:
                for cp in (to_core(q, rows), ring_copy(True, q, rows), ring_copy(False, 4 + q, rows)):
                    cp.wait_send()

        with jax.named_scope("bd"):
            back_caps(t, drained)
        for_each(t, lambda tt, rows: _wait(w_copies(tt, rows)))

        @pl.when(t > 2)
        def _():
            em_copy(t - 2).wait()

    _loop(step_count - 2, backward)
    weights(1)

    def rest(i):
        r = eight(kept // 8 + i)
        rc = rcs[1, r, :]
        live = lcol_ref[r, :] > 1
        for k in range(tiles):
            h, col = inner(k)
            val = emv[1, r, lane(k)].astype(F32) * rc
            strips[h, r, col] = jnp.where(live, val, 0.0).astype(BF16)

    _loop((seqs - kept) // 8, rest)
    _start(w_copies(1, caps[0]))
    _wait(w_copies(1, caps[0]))


def _run_recursion(nd, caps, ident, trans_loc, em, init_loc, lcol, lrow):
    step_count, seqs, bs = em.shape
    hb = bs // 2
    kept = max(caps[1:])
    depth = min(8 if kept < seqs else 4, bs // LANES)
    dma = pltpu.SemaphoreType.DMA
    two, credit = dma((2,)), pltpu.SemaphoreType.REGULAR((2,))
    vm, hbm = pl.BlockSpec(memory_space=pltpu.VMEM), pl.BlockSpec(memory_space=pl.ANY)
    scratch = [
        pltpu.VMEM((12, hb, bs), BF16),
        pltpu.VMEM((8, 2, seqs, hb), BF16),
        pltpu.VMEM((6, seqs, hb), F32),
        pltpu.VMEM((2, seqs, bs), BF16),
        pltpu.VMEM((step_count, seqs, LANES), F32),
        pltpu.VMEM((seqs, LANES), F32),
        pltpu.VMEM((8, seqs), F32),
        pltpu.VMEM((nd, 8, seqs), F32),
        pltpu.VMEM((depth, LANES, hb), BF16),
        pltpu.VMEM((2, kept, hb), F32),
        pltpu.VMEM((2, kept, hb), F32),
        pltpu.VMEM((2, kept, hb), F32),
        pltpu.VMEM((2, 2, kept, hb), F32),
        dma((12,)), two, dma((nd, 2)), dma((3, 2)), dma((nd, 2)), two, dma((nd,)), dma((nd,)), two,
        two, dma((depth,)), two, two, dma((6,)), two, dma((2, 2)), credit, credit, credit,
    ]
    return pl.pallas_call(
        functools.partial(_recursion, caps),
        name=f"recursion{ident}",
        out_shape=[
            jax.ShapeDtypeStruct((sum(caps), bs), BF16),
            jax.ShapeDtypeStruct((sum(caps), bs), BF16),
            jax.ShapeDtypeStruct((seqs, bs), F32),
            jax.ShapeDtypeStruct((8, seqs), F32),
            jax.ShapeDtypeStruct(trans_loc.shape, BF16),
        ],
        in_specs=[hbm, hbm, vm, vm, vm],
        out_specs=[hbm, hbm, hbm, vm, hbm],
        scratch_shapes=scratch,
        compiler_params=pltpu.CompilerParams(collective_id=ident, has_side_effects=True, vmem_limit_bytes=67_043_328),
    )(trans_loc, em, init_loc[None, :], lcol, lrow)


def _prepare(choices, tok_ref, len_ref, emt_hbm, em_hbm, lcol_ref, lrow_ref, rank_ref, level_ref,
             table, stable, picked, blocks, stage, table_sem, block_sem, stage_sem):
    step_count, seqs, bs = em_hbm.shape
    deep = blocks.shape[0]
    part = 32
    slab = min(512, bs)
    sub = lax.broadcasted_iota(jnp.int32, (seqs, LANES), 0)
    lan = lax.broadcasted_iota(jnp.int32, (seqs, LANES), 1)
    across = jnp.broadcast_to(len_ref[...].astype(F32), (seqs, seqs))
    down = jnp.transpose(across)
    ahead = (down > across) | ((down == across) & (sub < lan))
    rank = jnp.sum(jnp.where(ahead, 1.0, 0.0), axis=0, keepdims=True)
    rank_ref[...] = jnp.broadcast_to(rank, rank_ref.shape)
    pick = rank == sub.astype(F32)
    lcol = jnp.broadcast_to(jnp.sum(jnp.where(pick, across, 0.0), axis=1, keepdims=True), (seqs, LANES))
    lcol_ref[...] = lcol.astype(jnp.int32)
    lrow_ref[...] = jnp.transpose(lcol)[0:8].astype(jnp.int32)
    mat = jnp.zeros((seqs, LANES), F32)
    for t in range(step_count):
        tok = jnp.sum(jnp.where(pick, tok_ref[t : t + 1, :].astype(F32), 0.0), axis=1, keepdims=True)
        tok = jnp.broadcast_to(tok, (seqs, LANES))
        mat = jnp.where(lan == t, tok, mat)
        picked[t] = tok.astype(jnp.int32) & 7
    table[0:8] = jnp.transpose(mat)[0:8].astype(jnp.int32)
    alive = jnp.sum(jnp.where(across[0:8] > sub[0:8].astype(F32), 1.0, 0.0), axis=1, keepdims=True)
    table[8:16] = jnp.broadcast_to(alive, (8, LANES)).astype(jnp.int32)
    copy = pltpu.make_async_copy(table, stable, table_sem)
    copy.start()
    copy.wait()
    level = jnp.int32(0)
    for k, caps in enumerate(choices):
        for t in range(1, step_count):
            level = jnp.where(stable[8 + t, 0] > caps[t - 1], k + 1, level)
    level_ref[0] = level

    def parts(t):
        return (stable[8 + t, 0] + (part - 1)) // part

    def fetch(t):
        def body(p, carry):
            for k in range(part):
                s = p * part + k
                pltpu.make_async_copy(emt_hbm.at[stable[t, s] >> 3], blocks.at[t % deep, s], block_sem.at[t % deep]).start()
            return carry

        lax.fori_loop(0, parts(t), body, 0)

    def landed(t):
        def body(p, carry):
            pltpu.make_async_copy(emt_hbm.at[pl.ds(0, part)], blocks.at[t % deep, pl.ds(0, part)], block_sem.at[t % deep]).wait()
            return carry

        lax.fori_loop(0, parts(t), body, 0)

    def select(t):
        def body(p, carry):
            r = pl.ds(pl.multiple_of(p * part, part), part)
            at = picked[t, r, :] + 8 * sub[0:part]
            one = jnp.concatenate([jnp.where(lan[0:part] + off == at, 1.0, 0.0) for off in (0, LANES)], axis=1).astype(BF16)
            for n in range(bs // slab):
                cols = pl.ds(n * slab, slab)
                rows = blocks[t % deep, r, :, cols].reshape(part * 8, slab)
                stage[t % 2, r, cols] = _dot(one, rows).astype(BF16)
            return carry

        lax.fori_loop(0, parts(t), body, 0)

    def out_copy(t):
        return pltpu.make_async_copy(stage.at[t % 2], em_hbm.at[t], stage_sem.at[t % 2])

    def position(t):
        pl.when(t >= 2)(lambda: out_copy(t - 2).wait())
        landed(t)
        select(t)
        out_copy(t).start()
        pl.when(t + deep < step_count)(lambda: fetch(t + deep))

    _loop(deep, fetch)
    _loop(step_count, position)
    _loop(2, lambda e: out_copy(step_count - 1 - e).wait())


def _run_prepare(choices, tokens, lengths, emit_loc):
    bs, symbols = emit_loc.shape
    seqs, step_count = tokens.shape
    dma = pltpu.SemaphoreType.DMA
    vm, hbm = pl.BlockSpec(memory_space=pltpu.VMEM), pl.BlockSpec(memory_space=pl.ANY)
    return pl.pallas_call(
        functools.partial(_prepare, choices),
        name="prepare",
        out_shape=[
            jax.ShapeDtypeStruct((step_count, seqs, bs), BF16),
            jax.ShapeDtypeStruct((seqs, LANES), jnp.int32),
            jax.ShapeDtypeStruct((8, seqs), jnp.int32),
            jax.ShapeDtypeStruct((8, seqs), F32),
            jax.ShapeDtypeStruct((1,), jnp.int32),
        ],
        in_specs=[vm, vm, hbm],
        out_specs=[hbm, vm, vm, vm, pl.BlockSpec(memory_space=pltpu.SMEM)],
        scratch_shapes=[
            pltpu.VMEM((16, LANES), jnp.int32),
            pltpu.SMEM((16, LANES), jnp.int32),
            pltpu.VMEM((step_count, seqs, LANES), jnp.int32),
            pltpu.VMEM((4, seqs, 8, bs), BF16),
            pltpu.VMEM((2, seqs, bs), BF16),
            dma, dma((4,)), dma((2,)),
        ],
        compiler_params=pltpu.CompilerParams(vmem_limit_bytes=60_000_000),
    )(tokens.T, lengths[None, :], emit_loc.T.reshape(symbols // 8, 8, bs))


def _counts(trans_hbm, alpha_hbm, w_hbm, post_hbm, ll_ref, rank_ref, counts_hbm, posterior_hbm, loglik_ref,
            alpha, w, diag, out, post, back, in_sem, alpha_sem, diag_sem, out_sem, back_sem):
    rows, bs = w.shape
    seqs = post.shape[0]
    steps, tile, _ = diag.shape
    slab = min(512, bs)
    first = lax.axis_index(AXIS) * bs
    loads = [pltpu.make_async_copy(post_hbm, post, in_sem.at[0]), pltpu.make_async_copy(w_hbm, w, in_sem.at[1])]
    _start(loads)

    def alpha_copy(i):
        at = pl.multiple_of(i * tile, tile)
        return pltpu.make_async_copy(alpha_hbm.at[:, pl.ds(at, tile)], alpha.at[i], alpha_sem.at[i])

    def diag_copy(i):
        at = pl.multiple_of(first + i * tile, tile)
        return pltpu.make_async_copy(trans_hbm.at[pl.ds(at, tile)], diag.at[i], diag_sem.at[i])

    def out_copy(i):
        at = pl.multiple_of(i * tile, tile)
        return pltpu.make_async_copy(out.at[i], counts_hbm.at[pl.ds(at, tile)], out_sem.at[i])

    def bring(i):
        alpha_copy(i).start()
        diag_copy(i).start()

    _loop(steps, bring)

    rank = jnp.broadcast_to(rank_ref[0:1, :], (seqs, seqs))
    sub = lax.broadcasted_iota(jnp.int32, (seqs, seqs), 0).astype(F32)
    lan = lax.broadcasted_iota(jnp.int32, (seqs, seqs), 1).astype(F32)
    lls = jnp.transpose(jnp.broadcast_to(ll_ref[0:1, :], (seqs, seqs)))
    loglik_ref[...] = jnp.sum(jnp.where(rank == sub, lls, 0.0), axis=0, keepdims=True)
    order = jnp.where(jnp.transpose(rank) == lan, 1.0, 0.0).astype(BF16)
    loads[0].wait()
    for n in range(bs // slab):
        cols = pl.ds(n * slab, slab)
        rest = post[:, cols]
        total = jnp.zeros(rest.shape, F32)
        for _ in range(3):
            head = rest.astype(BF16)
            rest = rest - head.astype(F32)
            total = total + _dot(order, head)
        back[:, cols] = total
    back_copy = pltpu.make_async_copy(back, posterior_hbm, back_sem)
    back_copy.start()
    loads[1].wait()

    def step(i):
        alpha_copy(i).wait()
        lhs = alpha[i]
        diag_copy(i).wait()
        for n in range(bs // slab):
            cols = pl.ds(n * slab, slab)
            out[i, :, cols] = diag[i, :, cols].astype(F32) * _dot(lhs, w[:, cols], 0)
        out_copy(i).start()

    _loop(steps, step)
    _loop(steps, lambda i: out_copy(i).wait())
    back_copy.wait()


def _run_counts(alphas, ws, trans_loc, post, ll, rank):
    rows, bs = alphas.shape
    seqs = post.shape[0]
    tile = min(256, bs)
    steps = bs // tile
    dma = pltpu.SemaphoreType.DMA
    vm, hbm = pl.BlockSpec(memory_space=pltpu.VMEM), pl.BlockSpec(memory_space=pl.ANY)
    return pl.pallas_call(
        _counts,
        name="counts",
        out_shape=[
            jax.ShapeDtypeStruct((bs, bs), F32),
            jax.ShapeDtypeStruct((seqs, bs), F32),
            jax.ShapeDtypeStruct((1, seqs), F32),
        ],
        in_specs=[hbm, hbm, hbm, hbm, vm, vm],
        out_specs=[hbm, hbm, vm],
        scratch_shapes=[
            pltpu.VMEM((steps, rows, tile), BF16),
            pltpu.VMEM((rows, bs), BF16),
            pltpu.VMEM((steps, tile, bs), BF16),
            pltpu.VMEM((steps, tile, bs), F32),
            pltpu.VMEM((seqs, bs), F32),
            pltpu.VMEM((seqs, bs), F32),
            dma((2,)), dma((steps,)), dma((steps,)), dma((steps,)), dma,
        ],
        compiler_params=pltpu.CompilerParams(vmem_limit_bytes=60_000_000),
    )(trans_loc, alphas, ws, post, ll, rank)


def _capacities(seqs, step_count, spread):
    caps = []
    for t in range(1, step_count):
        live = (step_count - t) / step_count
        room = spread * math.sqrt((seqs - 1) * live * (1 - live))
        caps.append(min(seqs, 8 * math.ceil(((seqs - 1) * live + 1 + room) / 8)))
    return tuple(caps)


def solution(mesh):
    nd = mesh.shape[AXIS]

    def local_run(trans_loc, emit_loc, init_loc, tokens_loc, lengths_loc):
        seqs, step_count = tokens_loc.shape
        choices = [_capacities(seqs, step_count, spread) for spread in (2.7, 4.1)]
        em, lcol, lrow, rank, level = _run_prepare(choices, tokens_loc, lengths_loc, emit_loc)

        def run(ident, caps, trans, em, init, lcol, lrow, rank):
            alphas, ws, post, ll, _ = _run_recursion(nd, caps, ident, trans, em, init, lcol, lrow)
            return _run_counts(alphas, ws, trans, post, ll, rank)

        choices.append((seqs,) * (step_count - 1))
        runs = [functools.partial(run, k, caps) for k, caps in enumerate(choices)]
        counts, posterior, loglik = lax.switch(level[0], runs, trans_loc, em, init_loc, lcol, lrow, rank)
        return loglik[0], posterior, counts

    return jax.shard_map(
        local_run,
        mesh=mesh,
        in_specs=(P(None, AXIS), P(AXIS, None), P(AXIS), P("seqs", None), P("seqs")),
        out_specs=(P("seqs"), P("seqs", AXIS), P(("seqs", AXIS), None)),
        check_vma=False,
    )
```

profile of v0, /device:TPU:81, one launch (start us, length us, event | category | flops | bytes accessed | tf_op | source)
XLA Modules:
  0.0 343.3 jit_solution(10177139637594669799)
XLA Ops:
  0.6 15.2 %prepare.1 = (bf16[8,128,2048]{2,1,0:T(8,128)(2,1)}, s32[128,128]{1,0:T(8,128)}, s32[8,128]{1,0:T(8,128)}, f32[8,128]{1,0:T(8,128)}, s32[1]{0:T(128)}) custom-call(s32[8,128]{1,0:T(8,128)} %bitcast.13, s32[1,128]{1,0:T(1,128)} %bitcast.14, bf16[1250,8,2048]{2,1,0:T(8,128)(2,1)} %bitcast.12), custom_call_target="tpu_custom_call" | custom-call | tf_op jit(solution)/shard_map/prepare/pallas_call | solution.py:709
  16.4 326.7 %conditional.1 = (f32[2048,2048]{1,0:T(8,128)}, f32[128,2048]{1,0:T(8,128)}, f32[128]{0:T(128)}) conditional(s32[]{:T(128)} %bitcast.10, (f32[2048]{0:T(1024)}, bf16[16384,2048]{1,0:T(8,128)(2,1)}, bf16[8,128,2048]{2,1,0:T(8,128)(2,1)}, s32[128,128]{1,0:T(8,128)}, s32[8,128]{1,0:T(8,128)}, /*index=5*/f32[8,128]{1,0:T(8,128)}) %tuple.23, ...), branch_computations={%region_0.0_spmd, %region_1.0_spmd, %region_2.0_spmd} | conditional | bytes 24 | solution.py:848
  16.5 313.2 %recursion0.1 = (bf16[560,2048]{1,0:T(8,128)(2,1)}, bf16[560,2048]{1,0:T(8,128)(2,1)}, f32[128,2048]{1,0:T(8,128)}, f32[8,128]{1,0:T(8,128)}, bf16[16384,2048]{1,0:T(8,128)(2,1)}) custom-call(bf16[16384,2048]{1,0:T(8,128)(2,1)} %get-tuple-element.46.a_hbm.trans_hbm, bf16[8,128,2048]{2,1,0:T(8,128)(2,1)} %get-tuple-element.47.em_hbm, f32[1,2048]{1,0:T(1,128)} %bitcast.pi_ref, ...), custom_call_target="tpu_custom_call" | custom-call | tf_op jit(solution)/shard_map/cond/branch_0_fun/recursion0/pallas_call | solution.py:605
  329.7 13.2 %counts.3 = (f32[2048,2048]{1,0:T(8,128)}, f32[128,2048]{1,0:T(8,128)}, f32[1,128]{1,0:T(1,128)}) custom-call(bf16[16384,2048]{1,0:T(8,128)(2,1)} %get-tuple-element.46.a_hbm.trans_hbm, bf16[560,2048]{1,0:T(8,128)(2,1)} %get-tuple-element.51.alpha_hbm, bf16[560,2048]{1,0:T(8,128)(2,1)} %get-tuple-element.52.w_hbm, f32[128,2048]{1,0:T(8,128)} %get-tuple-element.53.post_hbm, ...), custom_call_target="tpu_custom_call" | custom-call | tf_op jit(solution)/shard_map/cond/branch_0_fun/counts/pallas_call | solution.py:802
where the time goes:
time: 343 us
  Pallas kernels  342 us (100%)
    pallas_call x1, Pallas kernels, _run_recursion(): pl.pallas_call(functools.partial(_recursion, caps), name=f'recursion{iden...  313 us
    pallas_call x1, Pallas kernels, _run_prepare(): pl.pallas_call(functools.partial(_prepare, choices), name='prepare', out_...  15.2 us
    pallas_call x1, Pallas kernels, _run_counts(): pl.pallas_call(_counts, name='counts', out_shape=[jax.ShapeDtypeStruct((b...  13.2 us

commit v1 on v0

--- a/solution.py
+++ b/solution.py
@@ -167,8 +167,6 @@
     barrier = pltpu.get_barrier_semaphore()
     for k in range(1, nd):
         pl.semaphore_signal(barrier, inc=1, device_id={AXIS: (g + k) % nd}, device_id_type=pl.DeviceIdType.MESH)
-    pl.semaphore_wait(barrier, nd - 1)
-
     tall = 16
 
     def rows_of(i):
@@ -236,7 +234,10 @@
 
     ll_ref[...] = jnp.zeros_like(ll_ref)
     for h in BOTH:
-        acc[h] = jnp.broadcast_to(pi_ref[:, h * hb : (h + 1) * hb], (seqs, hb))
+        acc[h] = jnp.broadcast_to(pi_ref[:, pl.ds(h * hb, hb)], (seqs, hb))
+    em_copy(0).wait()
+    weigh(0)
+    pl.semaphore_wait(barrier, nd - 1)
 
     def own_copies(rows):
         m = pl.ds(0, rows)
@@ -274,9 +275,6 @@
 
     def forward(t):
         pl.when(t > 0)(lambda: predict(t))
-        em_copy(t).wait()
-        with jax.named_scope("fw"):
-            weigh(t)
         normalise(t)
 
     def predict(t):
@@ -326,7 +324,7 @@
                 @pl.when(t == final)
                 def _():
                     load_turned(8 + i, 12 + i)
-                    load_turned(i, 4 + i)
+                    pl.when(k == 0)(lambda: load_turned(i, 4 + i))
 
             _loop(2, body)
 
@@ -365,7 +363,11 @@
         pl.when(t == 1)(lambda: _loop(4, lambda i: in_bank(4 + i)))
         with jax.named_scope("f3"):
             _loop(2, group3)
-        pl.when(t == final)(lambda: _loop(4, lambda i: load_turned(4 + i, 8 + i)))
+
+        @pl.when(t == final)
+        def _():
+            _loop(4, lambda i: load_turned(4 + i, 8 + i))
+            _loop(2, lambda i: load_turned(2 + i, 6 + i))
 
         def drained(rows):
             for cp in own_copies(rows):
@@ -378,6 +380,9 @@
 
         for_caps(t, drained)
         for_each(t, lambda tt, rows: _wait(save_copies(tt, rows)))
+        em_copy(t).wait()
+        with jax.named_scope("fw"):
+            weigh(t)
 
     _loop(step_count, forward)
 
@@ -406,151 +411,159 @@
         return [pltpu.make_async_copy(strips.at[h, pl.ds(0, rows)], w_hbm.at[to, pl.ds(h * hb, hb)], save_sem.at[h])
                 for h in BOTH]
 
-    def partial_sums(out, tile):
-        for n in range(hb // slab):
-            cols = pl.ds(n * slab, slab)
-            more = pl.ds(hb + n * slab, slab)
-            out[sent, cols] = _dot(strips[0, sent, :], tile[:, cols]) + _dot(strips[1, sent, :], tile[:, more])
-
-    def add_into(out, *terms):
+    sub = hb // 2
+
+    def part(s, base=0):
+        return pl.ds(pl.multiple_of(base + s * sub, sub), sub)
+
+    def partial_sums(out, tile, s):
+        out[sent, part(s)] = _dot(strips[0, sent, :], tile[:, part(s)]) + _dot(strips[1, sent, :], tile[:, part(s, hb)])
+
+    def add_into(out, s, *terms):
         def body(i):
             r = eight(i)
-            val = out[r, :]
+            val = out[r, part(s)]
             for term in terms:
-                val = val + term[r, :]
-            out[r, :] = val
+                val = val + term[r, part(s)]
+            out[r, part(s)] = val
 
         _loop(kept // 8, body)
 
-    def to_core(q, rows):
-        m = pl.ds(0, rows)
-        return remote(ost.at[q, m], dbuf.at[q, m], d_send.at[q], d_recv.at[q], partner)
-
-    def staged(p):
-        n, q = p // 2, p % 2
-        return (1 - n % 2) * (2 + n) + q
-
-    def ring_copy(far, p, rows):
-        m, q = pl.ds(0, rows), p % 2
-        to = dev(1 + (nx - 2) * q, 0)
-        src, send = work.at[staged(p), m], s_send.at[p]
-        if far:
-            return remote(src, trans.at[q, m], send, t_recv.at[q], to)
-        half = (p // 2 + q) % 2
-        return remote(src, fin.at[q, half, m], send, f_recv.at[q, half], to)
+    def to_core(q, s, rows):
+        at = (q, pl.ds(0, rows), part(s))
+        return remote(ost.at[at], dbuf.at[at], d_send.at[q, s], d_recv.at[q, s], partner)
+
+    def staged(n, q):
+        return work.at[(1 - n % 2) * (2 + n) + q]
+
+    def ring_copy(n, q, s, rows, dst, recv):
+        src = staged(n, q).at[pl.ds(0, rows), part(s)]
+        return remote(src, dst, s_send.at[2 * n + q, s], recv, dev(1 + (nx - 2) * q, 0))
+
+    def far_copy(q, s, rows):
+        return ring_copy(0, q, s, rows, trans.at[q, pl.ds(0, rows), part(s)], t_recv.at[q, s])
+
+    def near_copy(n, q, s, rows):
+        half = (n + q) % 2
+        return ring_copy(n, q, s, rows, fin.at[q, half, pl.ds(0, rows), part(s)], f_recv.at[q, half, s])
 
     def freed(sem, q):
-        pl.semaphore_signal(sem.at[q], inc=1, device_id={AXIS: dev(nx - 1 - (nx - 2) * q, 0)},
+        pl.semaphore_signal(sem, inc=1, device_id={AXIS: dev(nx - 1 - (nx - 2) * q, 0)},
                             device_id_type=pl.DeviceIdType.MESH)
 
     def backward(idx):
         t = step_count - 1 - idx
         with jax.named_scope("bw"):
             weights(t)
-        _loop(2, functools.partial(freed, f_free))
+        _loop(2, lambda q: freed(f_free.at[q], q))
         for_each(t, lambda tt, rows: _start(w_copies(tt, rows)))
 
         @pl.when(t > 2)
         def _():
             em_copy(t - 2).start()
 
-        def slot_of(p, flip):
-            n, q = p // 2, p % 2
+        def slot_of(n, q, flip):
             inner = ((n + 1) % 4) // 2
-            return inner == 0, (1 - inner) * (8 + 2 * flip + q) + inner * (4 * (1 - q) + 2 * (n - 1) + flip)
-
-        def products(n, flip, outs):
-            outer, _ = slot_of(2 * n, flip)
-            slots = [slot_of(2 * n + q, flip)[1] for q in BOTH]
-
-            @pl.when(outer | (idx == 0))
+            return (1 - inner) * (8 + 2 * flip + q) + inner * (4 * (1 - q) + 2 * (n - 1) + flip)
+
+        def products(n, s, flip, outs):
+            slots = [slot_of(n, q, flip) for q in BOTH]
+
+            @pl.when((s == 0) & ((n % 3 == 0) | (idx == 0)))
             def _():
                 for slot in slots:
                     in_bank(slot)
 
             for slot, out in zip(slots, outs):
-                partial_sums(out, bank.at[slot])
-
-            @pl.when(n == 0)
+                partial_sums(out, bank.at[slot], s)
+
+            @pl.when((s == 1) & (n == 0))
             def _():
                 for slot in slots:
                     load_turned(slot, slot - 8)
 
-            @pl.when((n == 3) & (t > 2))
+            @pl.when((s == 1) & (n == 3) & (t > 2))
             def _():
                 for slot in slots:
                     load_turned(slot, slot + 4)
 
-        def for_other(n):
+        def for_other(n, s):
             def drain(rows):
                 for q in BOTH:
-                    to_core(q, rows).wait_send()
+                    to_core(q, s, rows).wait_send()
 
             pl.when(n > 0)(lambda: back_caps(t, drain))
-            products(n, 1, [ost.at[q] for q in BOTH])
+            products(n, s, 1, [ost.at[q] for q in BOTH])
 
             @pl.when((n > 0) | (idx > 0))
             def _():
                 for q in BOTH:
-                    pl.semaphore_wait(d_free.at[q], 1)
-
-            back_caps(t, lambda rows: _start([to_core(q, rows) for q in BOTH]))
-
-        def for_this(n):
-            outs = [work.at[staged(2 * n + q)] for q in BOTH]
-            pl.when((n == 2) & (idx == 0))(lambda: _wait([post_copy(q) for q in BOTH]))
+                    pl.semaphore_wait(d_free.at[q, s], 1)
+
+            back_caps(t, lambda rows: _start([to_core(q, s, rows) for q in BOTH]))
+
+        def for_this(n, s):
+            outs = [staged(n, q) for q in BOTH]
+            pl.when((n == 2) & (idx == 0) & (s == 0))(lambda: _wait([post_copy(q) for q in BOTH]))
 
             def drain(rows):
                 for q in BOTH:
-                    ring_copy(False, 2 + q, rows).wait_send()
+                    near_copy(1, q, s, rows).wait_send()
 
             pl.when(n == 3)(lambda: back_caps(t, drain))
-            products(n, 0, outs)
-            for q, out in enumerate(outs):
-                p = 2 * n + q
-                back_caps(t, lambda rows: to_core(q, rows).wait_recv())
+            products(n, s, 0, outs)
+
+            def pass_on(q):
+                out = staged(n, q)
+                back_caps(t, lambda rows: to_core(q, s, rows).wait_recv())
 
                 @pl.when(n == 2)
                 def _():
-                    back_caps(t, lambda rows: ring_copy(True, q, rows).wait_recv())
-                    add_into(out, dbuf.at[q], trans.at[q])
-                    pl.when(t > 2)(lambda: freed(t_free, q))
-
-                pl.when(n != 2)(lambda: add_into(out, dbuf.at[q]))
+                    back_caps(t, lambda rows: far_copy(q, s, rows).wait_recv())
+                    add_into(out, s, dbuf.at[q], trans.at[q])
+                    pl.when(t > 2)(lambda: freed(t_free.at[q, s], q))
+
+                pl.when(n != 2)(lambda: add_into(out, s, dbuf.at[q]))
 
                 @pl.when((n < 3) | (t > 2))
                 def _():
-                    pl.semaphore_signal(d_free.at[q], inc=1, device_id={AXIS: partner}, device_id_type=pl.DeviceIdType.MESH)
+                    pl.semaphore_signal(d_free.at[q, s], inc=1, device_id={AXIS: partner}, device_id_type=pl.DeviceIdType.MESH)
 
                 @pl.when(n == 0)
                 def _():
-                    pl.when(idx > 0)(lambda: pl.semaphore_wait(t_free.at[q], 1))
-                    back_caps(t, lambda rows: ring_copy(True, q, rows).start())
+                    pl.when(idx > 0)(lambda: pl.semaphore_wait(t_free.at[q, s], 1))
+                    back_caps(t, lambda rows: far_copy(q, s, rows).start())
 
                 @pl.when((n == 1) | (n == 2))
                 def _():
-                    pl.when(n == 1)(lambda: pl.semaphore_wait(f_free.at[q], 1))
-                    back_caps(t, lambda rows: ring_copy(False, p, rows).start())
-
-        def stage(n):
+                    pl.when((n == 1) & (s == 0))(lambda: pl.semaphore_wait(f_free.at[q], 1))
+                    back_caps(t, lambda rows: near_copy(n, q, s, rows).start())
+
+            _loop(2, pass_on)
+
+        def stage(h):
+            n, s = h // 2, h % 2
             with jax.named_scope("bo"):
-                for_other(n)
+                for_other(n, s)
             with jax.named_scope("bt"):
-                for_this(n)
-
-        _loop(4, stage)
+                for_this(n, s)
+
+        _loop(8, stage)
 
         def landed(rows):
-            for p in range(2, 6):
-                ring_copy(False, p, rows).wait_recv()
+            for q in BOTH:
+                for s in BOTH:
+                    near_copy(1, q, s, rows).wait_recv()
+                    near_copy(2, q, s, rows).wait_recv()
 
         with jax.named_scope("bl"):
             back_caps(t, landed)
 
         def drained(rows):
             for q in BOTH:
-                for cp in (to_core(q, rows), ring_copy(True, q, rows), ring_copy(False, 4 + q, rows)):
-                    cp.wait_send()
+                for s in BOTH:
+                    for cp in (to_core(q, s, rows), far_copy(q, s, rows), near_copy(2, q, s, rows)):
+                        cp.wait_send()
 
         with jax.named_scope("bd"):
             back_caps(t, drained)
@@ -583,7 +596,8 @@
     kept = max(caps[1:])
     depth = min(8 if kept < seqs else 4, bs // LANES)
     dma = pltpu.SemaphoreType.DMA
-    two, credit = dma((2,)), pltpu.SemaphoreType.REGULAR((2,))
+    two, four = dma((2,)), dma((2, 2))
+    credit, credits = pltpu.SemaphoreType.REGULAR((2,)), pltpu.SemaphoreType.REGULAR((2, 2))
     vm, hbm = pl.BlockSpec(memory_space=pltpu.VMEM), pl.BlockSpec(memory_space=pl.ANY)
     scratch = [
         pltpu.VMEM((12, hb, bs), BF16),
@@ -600,7 +614,7 @@
         pltpu.VMEM((2, kept, hb), F32),
         pltpu.VMEM((2, 2, kept, hb), F32),
         dma((12,)), two, dma((nd, 2)), dma((3, 2)), dma((nd, 2)), two, dma((nd,)), dma((nd,)), two,
-        two, dma((depth,)), two, two, dma((6,)), two, dma((2, 2)), credit, credit, credit,
+        two, dma((depth,)), four, four, dma((6, 2)), four, dma((2, 2, 2)), credits, credit, credits,
     ]
     return pl.pallas_call(
         functools.partial(_recursion, caps),
@@ -737,8 +751,8 @@
     steps, tile, _ = diag.shape
     slab = min(512, bs)
     first = lax.axis_index(AXIS) * bs
-    loads = [pltpu.make_async_copy(post_hbm, post, in_sem.at[0]), pltpu.make_async_copy(w_hbm, w, in_sem.at[1])]
-    _start(loads)
+    post_load, w_load = (pltpu.make_async_copy(a, b, in_sem.at[k]) for k, (a, b) in enumerate(((post_hbm, post), (w_hbm, w))))
+    _start((post_load, w_load))
 
     def alpha_copy(i):
         at = pl.multiple_of(i * tile, tile)
@@ -764,7 +778,7 @@
     lls = jnp.transpose(jnp.broadcast_to(ll_ref[0:1, :], (seqs, seqs)))
     loglik_ref[...] = jnp.sum(jnp.where(rank == sub, lls, 0.0), axis=0, keepdims=True)
     order = jnp.where(jnp.transpose(rank) == lan, 1.0, 0.0).astype(BF16)
-    loads[0].wait()
+    post_load.wait()
     for n in range(bs // slab):
         cols = pl.ds(n * slab, slab)
         rest = post[:, cols]
@@ -776,7 +790,7 @@
         back[:, cols] = total
     back_copy = pltpu.make_async_copy(back, posterior_hbm, back_sem)
     back_copy.start()
-    loads[1].wait()
+    w_load.wait()
 
     def step(i):
         alpha_copy(i).wait()

time: 343 us -> 349 us (1.017)
  Pallas kernels: 342 us -> 347 us
    pallas_call x1, Pallas kernels: 313 us -> 320 us  [_run_recursion(): pl.pallas_call(functools.partial(_recursion, caps), name=f'recursion{iden...]
where the time goes in v1:
time: 349 us
  Pallas kernels  347 us (99%)
    pallas_call x1, Pallas kernels, _run_recursion(): pl.pallas_call(functools.partial(_recursion, caps), name=f'recursion{iden...  320 us
    pallas_call x1, Pallas kernels, _run_prepare(): pl.pallas_call(functools.partial(_prepare, choices), name='prepare', out_...  14.6 us
    pallas_call x1, Pallas kernels, _run_counts(): pl.pallas_call(_counts, name='counts', out_shape=[jax.ShapeDtypeStruct((b...  13.2 us

profile of v1, /device:TPU:81, one launch (start us, length us, event | category | flops | bytes accessed | tf_op | source)
XLA Modules:
  0.0 349.1 jit_solution(3306810564738631442)
XLA Ops:
  0.6 14.6 %prepare.1 = (bf16[8,128,2048]{2,1,0:T(8,128)(2,1)}, s32[128,128]{1,0:T(8,128)}, s32[8,128]{1,0:T(8,128)}, f32[8,128]{1,0:T(8,128)}, s32[1]{0:T(128)}) custom-call(s32[8,128]{1,0:T(8,128)} %bitcast.13, s32[1,128]{1,0:T(1,128)} %bitcast.14, bf16[1250,8,2048]{2,1,0:T(8,128)(2,1)} %bitcast.12), custom_call_target="tpu_custom_call" | custom-call | tf_op jit(solution)/shard_map/prepare/pallas_call | solution.py:723
  15.8 333.1 %conditional.1 = (f32[2048,2048]{1,0:T(8,128)}, f32[128,2048]{1,0:T(8,128)}, f32[128]{0:T(128)}) conditional(s32[]{:T(128)} %bitcast.10, (f32[2048]{0:T(1024)}, bf16[16384,2048]{1,0:T(8,128)(2,1)}, bf16[8,128,2048]{2,1,0:T(8,128)(2,1)}, s32[128,128]{1,0:T(8,128)}, s32[8,128]{1,0:T(8,128)}, /*index=5*/f32[8,128]{1,0:T(8,128)}) %tuple.23, ...), branch_computations={%region_0.0_spmd, %region_1.0_spmd, %region_2.0_spmd} | conditional | bytes 24 | solution.py:862
  15.9 319.6 %recursion0.1 = (bf16[560,2048]{1,0:T(8,128)(2,1)}, bf16[560,2048]{1,0:T(8,128)(2,1)}, f32[128,2048]{1,0:T(8,128)}, f32[8,128]{1,0:T(8,128)}, bf16[16384,2048]{1,0:T(8,128)(2,1)}) custom-call(bf16[16384,2048]{1,0:T(8,128)(2,1)} %get-tuple-element.46.a_hbm.trans_hbm, bf16[8,128,2048]{2,1,0:T(8,128)(2,1)} %get-tuple-element.47.em_hbm, f32[1,2048]{1,0:T(1,128)} %bitcast.pi_ref, ...), custom_call_target="tpu_custom_call" | custom-call | tf_op jit(solution)/shard_map/cond/branch_0_fun/recursion0/pallas_call | solution.py:619
  335.5 13.2 %counts.3 = (f32[2048,2048]{1,0:T(8,128)}, f32[128,2048]{1,0:T(8,128)}, f32[1,128]{1,0:T(1,128)}) custom-call(bf16[16384,2048]{1,0:T(8,128)(2,1)} %get-tuple-element.46.a_hbm.trans_hbm, bf16[560,2048]{1,0:T(8,128)(2,1)} %get-tuple-element.51.alpha_hbm, bf16[560,2048]{1,0:T(8,128)(2,1)} %get-tuple-element.52.w_hbm, f32[128,2048]{1,0:T(8,128)} %get-tuple-element.53.post_hbm, ...), custom_call_target="tpu_custom_call" | custom-call | tf_op jit(solution)/shard_map/cond/branch_0_fun/counts/pallas_call | solution.py:816

commit v2 on v0

--- a/solution.py
+++ b/solution.py
@@ -167,8 +167,6 @@
     barrier = pltpu.get_barrier_semaphore()
     for k in range(1, nd):
         pl.semaphore_signal(barrier, inc=1, device_id={AXIS: (g + k) % nd}, device_id_type=pl.DeviceIdType.MESH)
-    pl.semaphore_wait(barrier, nd - 1)
-
     tall = 16
 
     def rows_of(i):
@@ -236,7 +234,10 @@
 
     ll_ref[...] = jnp.zeros_like(ll_ref)
     for h in BOTH:
-        acc[h] = jnp.broadcast_to(pi_ref[:, h * hb : (h + 1) * hb], (seqs, hb))
+        acc[h] = jnp.broadcast_to(pi_ref[:, pl.ds(h * hb, hb)], (seqs, hb))
+    em_copy(0).wait()
+    weigh(0)
+    pl.semaphore_wait(barrier, nd - 1)
 
     def own_copies(rows):
         m = pl.ds(0, rows)
@@ -274,9 +275,6 @@
 
     def forward(t):
         pl.when(t > 0)(lambda: predict(t))
-        em_copy(t).wait()
-        with jax.named_scope("fw"):
-            weigh(t)
         normalise(t)
 
     def predict(t):
@@ -326,7 +324,7 @@
                 @pl.when(t == final)
                 def _():
                     load_turned(8 + i, 12 + i)
-                    load_turned(i, 4 + i)
+                    pl.when(k == 0)(lambda: load_turned(i, 4 + i))
 
             _loop(2, body)
 
@@ -365,7 +363,11 @@
         pl.when(t == 1)(lambda: _loop(4, lambda i: in_bank(4 + i)))
         with jax.named_scope("f3"):
             _loop(2, group3)
-        pl.when(t == final)(lambda: _loop(4, lambda i: load_turned(4 + i, 8 + i)))
+
+        @pl.when(t == final)
+        def _():
+            _loop(4, lambda i: load_turned(4 + i, 8 + i))
+            _loop(2, lambda i: load_turned(2 + i, 6 + i))
 
         def drained(rows):
             for cp in own_copies(rows):
@@ -378,6 +380,9 @@
 
         for_caps(t, drained)
         for_each(t, lambda tt, rows: _wait(save_copies(tt, rows)))
+        em_copy(t).wait()
+        with jax.named_scope("fw"):
+            weigh(t)
 
     _loop(step_count, forward)
 

time: 343 us -> 343 us (level)
  no operation moved by 1% of the time
where the time goes in v2:
time: 343 us
  Pallas kernels  341 us (99%)
    pallas_call x1, Pallas kernels, _run_recursion(): pl.pallas_call(functools.partial(_recursion, caps), name=f'recursion{iden...  313 us
    pallas_call x1, Pallas kernels, _run_prepare(): pl.pallas_call(functools.partial(_prepare, choices), name='prepare', out_...  14.4 us
    pallas_call x1, Pallas kernels, _run_counts(): pl.pallas_call(_counts, name='counts', out_shape=[jax.ShapeDtypeStruct((b...  13.2 us

profile of v2, /device:TPU:81, one launch (start us, length us, event | category | flops | bytes accessed | tf_op | source)
XLA Modules:
  0.0 342.5 jit_solution(9499721327964841190)
XLA Ops:
  0.6 14.4 %prepare.1 = (bf16[8,128,2048]{2,1,0:T(8,128)(2,1)}, s32[128,128]{1,0:T(8,128)}, s32[8,128]{1,0:T(8,128)}, f32[8,128]{1,0:T(8,128)}, s32[1]{0:T(128)}) custom-call(s32[8,128]{1,0:T(8,128)} %bitcast.13, s32[1,128]{1,0:T(1,128)} %bitcast.14, bf16[1250,8,2048]{2,1,0:T(8,128)(2,1)} %bitcast.12), custom_call_target="tpu_custom_call" | custom-call | tf_op jit(solution)/shard_map/prepare/pallas_call | solution.py:714
  15.7 326.6 %conditional.1 = (f32[2048,2048]{1,0:T(8,128)}, f32[128,2048]{1,0:T(8,128)}, f32[128]{0:T(128)}) conditional(s32[]{:T(128)} %bitcast.10, (f32[2048]{0:T(1024)}, bf16[16384,2048]{1,0:T(8,128)(2,1)}, bf16[8,128,2048]{2,1,0:T(8,128)(2,1)}, s32[128,128]{1,0:T(8,128)}, s32[8,128]{1,0:T(8,128)}, /*index=5*/f32[8,128]{1,0:T(8,128)}) %tuple.23, ...), branch_computations={%region_0.0_spmd, %region_1.0_spmd, %region_2.0_spmd} | conditional | bytes 24 | solution.py:853
  15.7 313.2 %recursion0.1 = (bf16[560,2048]{1,0:T(8,128)(2,1)}, bf16[560,2048]{1,0:T(8,128)(2,1)}, f32[128,2048]{1,0:T(8,128)}, f32[8,128]{1,0:T(8,128)}, bf16[16384,2048]{1,0:T(8,128)(2,1)}) custom-call(bf16[16384,2048]{1,0:T(8,128)(2,1)} %get-tuple-element.46.a_hbm.trans_hbm, bf16[8,128,2048]{2,1,0:T(8,128)(2,1)} %get-tuple-element.47.em_hbm, f32[1,2048]{1,0:T(1,128)} %bitcast.pi_ref, ...), custom_call_target="tpu_custom_call" | custom-call | tf_op jit(solution)/shard_map/cond/branch_0_fun/recursion0/pallas_call | solution.py:610
  328.9 13.2 %counts.3 = (f32[2048,2048]{1,0:T(8,128)}, f32[128,2048]{1,0:T(8,128)}, f32[1,128]{1,0:T(1,128)}) custom-call(bf16[16384,2048]{1,0:T(8,128)(2,1)} %get-tuple-element.46.a_hbm.trans_hbm, bf16[560,2048]{1,0:T(8,128)(2,1)} %get-tuple-element.51.alpha_hbm, bf16[560,2048]{1,0:T(8,128)(2,1)} %get-tuple-element.52.w_hbm, f32[128,2048]{1,0:T(8,128)} %get-tuple-element.53.post_hbm, ...), custom_call_target="tpu_custom_call" | custom-call | tf_op jit(solution)/shard_map/cond/branch_0_fun/counts/pallas_call | solution.py:807
